TPU v7x, 32 devices: a whole 2x2x4 slice. The times are simulated.
32 devices in a mesh: shard: 4 (over x, core), owner: 8 (over z, y).
Axes of the slice: x: 2, y: 2, z: 4, core: 2. Of those that a mesh axis runs over, the one named last changes fastest.
Arguments:
- gradient: float32 [32, 2048, 768], P('owner', 'shard'), may hold values from -6 to 6
- old_basis: float32 [32, 2048, 256], P('owner', 'shard'), may hold values from -0.125 to 0.125
- moment_one: float32 [32, 256, 768], P('owner', 'shard'), may hold values from -6 to 6
- moment_two: float32 [32, 256, 768], P('owner', 'shard'), may hold values from 0.01 to 1
- slot_expert: int32 [32], replicated, may hold values from 0 to 31, as said below
- cost: int32 [32], replicated, may hold values from 0 to 5
Outputs:
- new_basis: float32 [32, 2048, 256], P('owner', 'shard')
- new_moment_one: float32 [32, 256, 768], P('owner', 'shard')
- new_moment_two: float32 [32, 256, 768], P('owner', 'shard')
- update: bfloat16 [32, 2048, 768], P('owner', 'shard')
Inputs may be any that keep to these rules, and one draw needn't show every extreme that they name: `slot_expert`: A permutation of the 32 experts. Expert e's gradient lies in owner group e // 4; state slot s lies in owner group s // 4. The 4 slots of one owner group hold experts of 4 different owner groups, and the 4 experts of one owner group are held by 4 different owner groups.
All inputs are finite; a program needn't handle non-finite values.
Results may differ from a plain program's by a relative error of at most 0.001.
Values sent between devices are 32-bit elements; how exact they have to be, the bound alone decides.
No kernel may reach another device: no remote copies, remote signals or barrier semaphores. Data moves between devices by JAX's collectives and lax.ppermute only.
A program may use at most 192 MiB of HBM per device.

v0:
```python
import jax
import jax.numpy as jnp
from jax import lax
from jax.sharding import PartitionSpec as P

HIGHEST_PREC = lax.Precision.HIGHEST
BETA_ONE = 0.9
BETA_TWO = 0.99
EPSILON = 1e-08
GALORE_SCALE = 0.25


def whole_step(basis_now, grad_now):
    inner_prod = jnp.dot(grad_now.T, basis_now, precision=HIGHEST_PREC)
    tall_block = jnp.dot(grad_now, inner_prod, precision=HIGHEST_PREC)
    gram_matrix = jnp.dot(tall_block.T, tall_block, precision=HIGHEST_PREC)
    factor = jnp.linalg.cholesky(gram_matrix)
    return lax.linalg.triangular_solve(
        factor, tall_block, left_side=False, lower=True, transpose_a=True
    )


def refresh_project(grad_slices, basis_slices, counts):
    slots = grad_slices.shape[0]
    grad_whole, basis_whole = (
        lax.all_to_all(grad_slices, "shard", split_axis=0, concat_axis=1, tiled=True),
        lax.all_to_all(basis_slices, "shard", split_axis=0, concat_axis=1, tiled=True),
    )
    shard_now = lax.axis_index("shard")
    my_count = jnp.sum(jnp.where(jnp.arange(slots) == shard_now, counts, 0))
    grad_now = grad_whole[0]
    basis_new = lax.fori_loop(
        0, my_count, lambda step_index, current: whole_step(current, grad_now), basis_whole[0]
    )
    projected = jnp.dot(basis_new.T, grad_now, precision=HIGHEST_PREC)
    basis_back, proj_back = (
        lax.all_to_all(basis_new[None], "shard", split_axis=1, concat_axis=0, tiled=True),
        lax.all_to_all(projected[None], "shard", split_axis=1, concat_axis=0, tiled=True),
    )
    return (basis_back, proj_back)


def on_device(gradient, old_basis, moment_one, moment_two, slot_expert, cost):
    slots = gradient.shape[0]
    owners = lax.axis_size("owner")
    owner_now = lax.axis_index("owner")
    table = slot_expert.reshape(owners, slots)
    mine = lax.dynamic_index_in_dim(table, owner_now, 0, keepdims=False)
    home_pick = (mine[:, None] // slots == jnp.arange(owners)[None, :]).astype(jnp.float32)
    own_ids = owner_now * slots + jnp.arange(slots)
    send_pick = jnp.sum((table[:, :, None] == own_ids[None, None, :]).astype(jnp.float32), axis=1)
    home_counts = lax.dynamic_slice_in_dim(cost, owner_now * slots, slots)
    outgoing = jnp.einsum("jh,jrq->hrq", home_pick, old_basis, precision=HIGHEST_PREC)
    arrived = lax.all_to_all(outgoing, "owner", split_axis=0, concat_axis=0, tiled=True)
    home_basis = jnp.einsum("oi,orq->irq", send_pick, arrived, precision=HIGHEST_PREC)
    basis_home, proj_home = refresh_project(gradient, home_basis, home_counts)
    basis_send = jnp.einsum("oi,irq->orq", send_pick, basis_home, precision=HIGHEST_PREC)
    proj_send = jnp.einsum("oi,iqc->oqc", send_pick, proj_home, precision=HIGHEST_PREC)
    basis_recv, proj_recv = (
        lax.all_to_all(basis_send, "owner", split_axis=0, concat_axis=0, tiled=True),
        lax.all_to_all(proj_send, "owner", split_axis=0, concat_axis=0, tiled=True),
    )
    basis_slot = jnp.einsum("jh,hrq->jrq", home_pick, basis_recv, precision=HIGHEST_PREC)
    projected = jnp.einsum("jh,hqc->jqc", home_pick, proj_recv, precision=HIGHEST_PREC)
    moment_new = BETA_ONE * moment_one + (1.0 - BETA_ONE) * projected
    second_new = BETA_TWO * moment_two + (1.0 - BETA_TWO) * projected * projected
    normed = moment_new / (jnp.sqrt(second_new) + EPSILON)
    expanded = jnp.einsum(
        "krq,kqc->krc",
        basis_slot,
        lax.all_gather(normed, "shard", axis=1, tiled=True),
        precision=HIGHEST_PREC,
    )
    update = (GALORE_SCALE * expanded).astype(jnp.bfloat16)
    return (basis_slot, moment_new, second_new, update)


def solution(mesh):
    in_specs = (
        P("owner", "shard", None),
        P("owner", "shard", None),
        P("owner", "shard", None),
        P("owner", "shard", None),
        P(),
        P(),
    )
    out_specs = (
        P("owner", "shard", None),
        P("owner", "shard", None),
        P("owner", "shard", None),
        P("owner", "shard", None),
    )
    return jax.shard_map(
        on_device, mesh=mesh, in_specs=in_specs, out_specs=out_specs, check_vma=False
    )
```

profile of v0, /device:TPU:0, one launch (start us, length us, event | category | flops | bytes accessed | tf_op | source)
XLA Modules:
  0.0 917.1 jit_solution(16307734282005896997)
XLA Ops:
  23.4 93.0 %all-to-all-done = f32[8,512,256]{2,1,0:T(8,128)} async-done(((f32[8,512,256]{2,1,0:T(8,128)}), f32[8,512,256]{2,1,0:T(8,128)}, u32[]{:S(2)}, u32[]{:S(2)}) %all-to-all-start) | async-done | bytes 4194336 | tf_op jit(solution)/shard_map/all_to_all | solution.py:54
  125.0 28.9 %all_to_all.57 = f32[4,512,256]{2,1,0:T(8,128)} all-to-all(f32[4,512,256]{2,1,0:T(8,128)S(1)} %copy.76), channel_id=1, replica_groups=mesh['shard'=4,'owner'=8] {'shard'}, dimensions={0} | all-to-all | bytes 4194304 | tf_op jit(solution)/shard_map/all_to_all | solution.py:27
  162.0 68.0 %all-to-all-done.2 = f32[4,512,768]{2,1,0:T(8,128)} async-done(((f32[4,512,768]{2,1,0:T(8,128)}), f32[4,512,768]{2,1,0:T(8,128)}, u32[]{:S(2)}, u32[]{:S(2)}) %all-to-all-start.2) | async-done | bytes 6291488 | tf_op jit(solution)/shard_map/all_to_all | solution.py:26
  230.0 453.1 %while.13 = (s32[]{:T(128)}, f32[2048,256]{0,1:T(8,128)S(1)}, s32[]{:T(128)}, f32[2048,768]{1,0:T(8,128)}, s32[]{:T(128)}, /*index=5*/s32[]{:T(128)}, f32[]{:T(128)}, s32[]{:T(128)}) while((s32[]{:T(128)}, f32[2048,256]{0,1:T(8,128)S(1)}, s32[]{:T(128)}, f32[2048,768]{1,0:T(8,128)}, s32[]{:T(128)}, /*index=5*/s32[]{:T(128)}, f32[]{:T(128)}, ...), condition=%wide.region_7.8_spmd, body=%wide.region_2.7_spmd.sunk | while | flops 12533907456 | bytes 35653912 | solution.py:32
  231.0 12.0 %fusion.84 = f32[768,256]{1,0:T(8,128)S(1)} fusion(f32[2048,768]{1,0:T(8,128)} %get-tuple-element.217, f32[2048,256]{0,1:T(8,128)S(1)} %get-tuple-element.207), kind=kOutput, calls=%fused_computation.65.clone.1 | convolution fusion | flops 4831838208 | bytes 9175040 | tf_op jit(solution)/shard_map/while/body/dot_general | solution.py:14
  243.1 12.7 %fusion.85 = f32[256,2048]{1,0:T(8,128)S(1)} fusion(f32[768,256]{1,0:T(8,128)S(1)} %fusion.84, f32[2048,768]{1,0:T(8,128)} %get-tuple-element.217), kind=kOutput, calls=%fused_computation.66.clone.1 | convolution fusion | flops 4831838208 | bytes 9175040 | tf_op jit(solution)/shard_map/while/body/dot_general | solution.py:15
  257.8 11.7 %cholesky.185 = f32[128,128]{1,0:T(8,128)S(1)} custom-call(f32[128,128]{1,0:T(8,128)S(1)} %cholesky.184), custom_call_target="Cholesky" | custom-call | tf_op jit(solution)/shard_map/while/body/jit(cholesky)/cholesky | solution.py:17
  279.9 11.7 %cholesky.187 = f32[128,128]{1,0:T(8,128)S(1)} custom-call(f32[128,128]{1,0:T(8,128)S(1)} %convolution_subtract_fusion.4), custom_call_target="Cholesky" | custom-call | tf_op jit(solution)/shard_map/while/body/jit(cholesky)/cholesky | solution.py:17
  297.7 19.7 %custom-call.20 = f32[2,128,128]{1,2,0:T(8,128)S(1)} custom-call(f32[2,128,128]{2,1,0:T(8,128)S(1)} %get-tuple-element.175), custom_call_target="InvertDiagBlocksLowerTriangular" | custom-call | tf_op jit(solution)/shard_map/while/body/triangular_solve | solution.py:18
  321.4 12.0 %fusion.84 = f32[768,256]{1,0:T(8,128)S(1)} fusion(f32[2048,768]{1,0:T(8,128)} %get-tuple-element.217, f32[2048,256]{0,1:T(8,128)S(1)} %get-tuple-element.207), kind=kOutput, calls=%fused_computation.65.clone.1 | convolution fusion | flops 4831838208 | bytes 9175040 | tf_op jit(solution)/shard_map/while/body/dot_general | solution.py:14
  333.4 12.7 %fusion.85 = f32[256,2048]{1,0:T(8,128)S(1)} fusion(f32[768,256]{1,0:T(8,128)S(1)} %fusion.84, f32[2048,768]{1,0:T(8,128)} %get-tuple-element.217), kind=kOutput, calls=%fused_computation.66.clone.1 | convolution fusion | flops 4831838208 | bytes 9175040 | tf_op jit(solution)/shard_map/while/body/dot_general | solution.py:15
  348.2 11.7 %cholesky.185 = f32[128,128]{1,0:T(8,128)S(1)} custom-call(f32[128,128]{1,0:T(8,128)S(1)} %cholesky.184), custom_call_target="Cholesky" | custom-call | tf_op jit(solution)/shard_map/while/body/jit(cholesky)/cholesky | solution.py:17
  370.3 11.7 %cholesky.187 = f32[128,128]{1,0:T(8,128)S(1)} custom-call(f32[128,128]{1,0:T(8,128)S(1)} %convolution_subtract_fusion.4), custom_call_target="Cholesky" | custom-call | tf_op jit(solution)/shard_map/while/body/jit(cholesky)/cholesky | solution.py:17
  388.1 19.7 %custom-call.20 = f32[2,128,128]{1,2,0:T(8,128)S(1)} custom-call(f32[2,128,128]{2,1,0:T(8,128)S(1)} %get-tuple-element.175), custom_call_target="InvertDiagBlocksLowerTriangular" | custom-call | tf_op jit(solution)/shard_map/while/body/triangular_solve | solution.py:18
  411.8 12.0 %fusion.84 = f32[768,256]{1,0:T(8,128)S(1)} fusion(f32[2048,768]{1,0:T(8,128)} %get-tuple-element.217, f32[2048,256]{0,1:T(8,128)S(1)} %get-tuple-element.207), kind=kOutput, calls=%fused_computation.65.clone.1 | convolution fusion | flops 4831838208 | bytes 9175040 | tf_op jit(solution)/shard_map/while/body/dot_general | solution.py:14
  423.8 12.7 %fusion.85 = f32[256,2048]{1,0:T(8,128)S(1)} fusion(f32[768,256]{1,0:T(8,128)S(1)} %fusion.84, f32[2048,768]{1,0:T(8,128)} %get-tuple-element.217), kind=kOutput, calls=%fused_computation.66.clone.1 | convolution fusion | flops 4831838208 | bytes 9175040 | tf_op jit(solution)/shard_map/while/body/dot_general | solution.py:15
  438.5 11.7 %cholesky.185 = f32[128,128]{1,0:T(8,128)S(1)} custom-call(f32[128,128]{1,0:T(8,128)S(1)} %cholesky.184), custom_call_target="Cholesky" | custom-call | tf_op jit(solution)/shard_map/while/body/jit(cholesky)/cholesky | solution.py:17
  460.6 11.7 %cholesky.187 = f32[128,128]{1,0:T(8,128)S(1)} custom-call(f32[128,128]{1,0:T(8,128)S(1)} %convolution_subtract_fusion.4), custom_call_target="Cholesky" | custom-call | tf_op jit(solution)/shard_map/while/body/jit(cholesky)/cholesky | solution.py:17
  478.4 19.7 %custom-call.20 = f32[2,128,128]{1,2,0:T(8,128)S(1)} custom-call(f32[2,128,128]{2,1,0:T(8,128)S(1)} %get-tuple-element.175), custom_call_target="InvertDiagBlocksLowerTriangular" | custom-call | tf_op jit(solution)/shard_map/while/body/triangular_solve | solution.py:18
  502.2 12.0 %fusion.84 = f32[768,256]{1,0:T(8,128)S(1)} fusion(f32[2048,768]{1,0:T(8,128)} %get-tuple-element.217, f32[2048,256]{0,1:T(8,128)S(1)} %get-tuple-element.207), kind=kOutput, calls=%fused_computation.65.clone.1 | convolution fusion | flops 4831838208 | bytes 9175040 | tf_op jit(solution)/shard_map/while/body/dot_general | solution.py:14
  514.2 12.7 %fusion.85 = f32[256,2048]{1,0:T(8,128)S(1)} fusion(f32[768,256]{1,0:T(8,128)S(1)} %fusion.84, f32[2048,768]{1,0:T(8,128)} %get-tuple-element.217), kind=kOutput, calls=%fused_computation.66.clone.1 | convolution fusion | flops 4831838208 | bytes 9175040 | tf_op jit(solution)/shard_map/while/body/dot_general | solution.py:15
  528.9 11.7 %cholesky.185 = f32[128,128]{1,0:T(8,128)S(1)} custom-call(f32[128,128]{1,0:T(8,128)S(1)} %cholesky.184), custom_call_target="Cholesky" | custom-call | tf_op jit(solution)/shard_map/while/body/jit(cholesky)/cholesky | solution.py:17
  551.0 11.7 %cholesky.187 = f32[128,128]{1,0:T(8,128)S(1)} custom-call(f32[128,128]{1,0:T(8,128)S(1)} %convolution_subtract_fusion.4), custom_call_target="Cholesky" | custom-call | tf_op jit(solution)/shard_map/while/body/jit(cholesky)/cholesky | solution.py:17
  568.8 19.7 %custom-call.20 = f32[2,128,128]{1,2,0:T(8,128)S(1)} custom-call(f32[2,128,128]{2,1,0:T(8,128)S(1)} %get-tuple-element.175), custom_call_target="InvertDiagBlocksLowerTriangular" | custom-call | tf_op jit(solution)/shard_map/while/body/triangular_solve | solution.py:18
  592.5 12.0 %fusion.84 = f32[768,256]{1,0:T(8,128)S(1)} fusion(f32[2048,768]{1,0:T(8,128)} %get-tuple-element.217, f32[2048,256]{0,1:T(8,128)S(1)} %get-tuple-element.207), kind=kOutput, calls=%fused_computation.65.clone.1 | convolution fusion | flops 4831838208 | bytes 9175040 | tf_op jit(solution)/shard_map/while/body/dot_general | solution.py:14
  604.5 12.7 %fusion.85 = f32[256,2048]{1,0:T(8,128)S(1)} fusion(f32[768,256]{1,0:T(8,128)S(1)} %fusion.84, f32[2048,768]{1,0:T(8,128)} %get-tuple-element.217), kind=kOutput, calls=%fused_computation.66.clone.1 | convolution fusion | flops 4831838208 | bytes 9175040 | tf_op jit(solution)/shard_map/while/body/dot_general | solution.py:15
  641.4 11.7 %cholesky.187 = f32[128,128]{1,0:T(8,128)S(1)} custom-call(f32[128,128]{1,0:T(8,128)S(1)} %convolution_subtract_fusion.4), custom_call_target="Cholesky" | custom-call | tf_op jit(solution)/shard_map/while/body/jit(cholesky)/cholesky | solution.py:17
  659.2 19.7 %custom-call.20 = f32[2,128,128]{1,2,0:T(8,128)S(1)} custom-call(f32[2,128,128]{2,1,0:T(8,128)S(1)} %get-tuple-element.175), custom_call_target="InvertDiagBlocksLowerTriangular" | custom-call | tf_op jit(solution)/shard_map/while/body/triangular_solve | solution.py:18
  714.9 21.8 %all-to-all-done.3 = f32[1,2048,256]{2,0,1:T(1,128)S(1)} async-done(((f32[1,2048,256]{2,0,1:T(1,128)}), f32[1,2048,256]{2,0,1:T(1,128)S(1)}, u32[]{:S(2)}, u32[]{:S(2)}) %all-to-all-start.3) | async-done | bytes 2097184 | tf_op jit(solution)/shard_map/all_to_all | solution.py:37
  736.7 21.8 %all-to-all-start.6 = ((f32[8,64,768]{2,1,0:T(8,128)}), f32[8,64,768]{2,1,0:T(8,128)}, u32[]{:S(2)}, u32[]{:S(2)}) async-start(f32[8,64,768]{2,1,0:T(8,128)} %copy.85), calls=%async_computation.6 | async-start | bytes 3145728 | tf_op jit(solution)/shard_map/all_to_all | solution.py:61
  767.4 27.7 %all-to-all-done.6 = f32[8,64,768]{2,1,0:T(8,128)} async-done(((f32[8,64,768]{2,1,0:T(8,128)}), f32[8,64,768]{2,1,0:T(8,128)}, u32[]{:S(2)}, u32[]{:S(2)}) %all-to-all-start.6) | async-done | bytes 1572896 | tf_op jit(solution)/shard_map/all_to_all | solution.py:61
  807.7 84.1 %all-to-all-done.4 = f32[8,512,256]{2,1,0:T(8,128)} async-done(((f32[8,512,256]{2,1,0:T(8,128)}), f32[8,512,256]{2,1,0:T(8,128)}, u32[]{:S(2)}, u32[]{:S(2)}) %all-to-all-start.4) | async-done | bytes 4194336 | tf_op jit(solution)/shard_map/all_to_all | solution.py:60
  (174 shorter events, 238.0 us)
Async XLA Ops:
  7.2 1.6 copy-start
  15.7 100.8 %all-to-all-start = ((f32[8,512,256]{2,1,0:T(8,128)}), f32[8,512,256]{2,1,0:T(8,128)}, u32[]{:S(2)}, u32[]{:S(2)}) async-start(f32[8,512,256]{2,1,0:T(8,128)} %copy.74), calls=%async_computation | async-start | bytes 8388608 | tf_op jit(solution)/shard_map/all_to_all | solution.py:54
  153.9 5.4 copy-start.2
  153.9 76.0 %all-to-all-start.2 = ((f32[4,512,768]{2,1,0:T(8,128)}), f32[4,512,768]{2,1,0:T(8,128)}, u32[]{:S(2)}, u32[]{:S(2)}) async-start(f32[4,512,768]{2,1,0:T(8,128)} %param.8), calls=%async_computation.2 | async-start | bytes 12582912 | tf_op jit(solution)/shard_map/all_to_all | solution.py:26
  692.3 15.1 %all-to-all-start.5 = ((f32[1,256,768]{2,0,1:T(1,128)}), f32[1,256,768]{2,0,1:T(1,128)S(1)}, u32[]{:S(2)}, u32[]{:S(2)}) async-start(f32[1,256,768]{2,0,1:T(1,128)} %copy.83), calls=%async_computation.5 | async-start | bytes 1572864 | tf_op jit(solution)/shard_map/all_to_all | solution.py:38
  707.4 29.3 %all-to-all-start.3 = ((f32[1,2048,256]{2,0,1:T(1,128)}), f32[1,2048,256]{2,0,1:T(1,128)S(1)}, u32[]{:S(2)}, u32[]{:S(2)}) async-start(f32[1,2048,256]{2,0,1:T(1,128)} %copy.94), calls=%async_computation.3 | async-start | bytes 4194304 | tf_op jit(solution)/shard_map/all_to_all | solution.py:37
  736.7 58.5 %all-to-all-start.6 = ((f32[8,64,768]{2,1,0:T(8,128)}), f32[8,64,768]{2,1,0:T(8,128)}, u32[]{:S(2)}, u32[]{:S(2)}) async-start(f32[8,64,768]{2,1,0:T(8,128)} %copy.85), calls=%async_computation.6 | async-start | bytes 3145728 | tf_op jit(solution)/shard_map/all_to_all | solution.py:61
  767.4 32.6 %copy-start.3 = (f32[4,64,768]{2,1,0:T(8,128)S(1)}, f32[4,64,768]{2,1,0:T(8,128)}, u32[]{:S(2)}) copy-start(f32[4,64,768]{2,1,0:T(8,128)} %param.11) | copy-start | bytes 2359300
  795.2 96.6 %all-to-all-start.4 = ((f32[8,512,256]{2,1,0:T(8,128)}), f32[8,512,256]{2,1,0:T(8,128)}, u32[]{:S(2)}, u32[]{:S(2)}) async-start(f32[8,512,256]{2,1,0:T(8,128)} %copy.80), calls=%async_computation.4 | async-start | bytes 8388608 | tf_op jit(solution)/shard_map/all_to_all | solution.py:60
  799.7 100.3 %all-gather.2.cloned.1.call-start = ((), (), s32[]{:S(2)}) async-start(), calls=%async_computation.7 | async-start | bytes 3932160 | tf_op jit(solution)/shard_map/all_gather | solution.py:71
  900.0 10.0 %copy-start.1 = (f32[4,512,256]{2,1,0:T(8,128)S(1)}, f32[4,512,256]{2,1,0:T(8,128)}, u32[]{:S(2)}) copy-start(f32[4,512,256]{2,1,0:T(8,128)} %param.9) | copy-start | bytes 6291460
Sparse Core Ops, SparseCore 0:
  805.8 29.1 all-gather.1
where the time goes:
time: 922 us; the launch traced here: 917 us
  waiting for transfers between devices  303 us (33%)
  other arithmetic  270 us (29%)
  matrix products  200 us (22%)
  starting transfers between devices  46.6 us (5%)
  local copies, waits for them, and re-layouts  42.2 us (5%)
  blocking collectives  28.9 us (3%)
  between operations  14.5 us (2%)
  loops' own time  11.9 us (1%)
    another operation x30, other arithmetic, whole_step(): factor = jnp.linalg.cholesky(gram_matrix)  170 us
    another operation x20, other arithmetic, whole_step(): lax.linalg.triangular_solve(factor, tall_block, left_side=False, lower=Tr...  99.3 us
    all_to_all x1, waiting for transfers between devices, on_device(): lax.all_to_all(outgoing, 'owner', split_axis=0, concat_axis=0, tiled=True)  93 us
    all_to_all x1, waiting for transfers between devices, on_device(): lax.all_to_all(basis_send, 'owner', split_axis=0, concat_axis=0, tiled=True)  84.1 us
    all_to_all x1, waiting for transfers between devices, refresh_project(): lax.all_to_all(grad_slices, 'shard', split_axis=0, concat_axis=1, tiled=T...  68 us
    dot_general x5, matrix products, whole_step(): tall_block = jnp.dot(grad_now, inner_prod, precision=HIGHEST_PREC)  63.3 us
    dot_general x5, matrix products, whole_step(): inner_prod = jnp.dot(grad_now.T, basis_now, precision=HIGHEST_PREC)  60.1 us
    all_to_all x1, blocking collectives, refresh_project(): lax.all_to_all(basis_slices, 'shard', split_axis=0, concat_axis=1, tiled=...  28.9 us
  transfers between devices with their start and end apart: 7, of which 6 were waited for; matrix products, arithmetic and copies ran while one was open for 4% of the time, Pallas kernels for 0%

commit v1 on v0

v1 whole, which is shorter than its diff:
```python
import functools

import jax
import jax.numpy as jnp
from jax import lax
from jax.experimental import pallas as pl
from jax.experimental.pallas import tpu as pltpu
from jax.sharding import PartitionSpec as P

HIGHEST_PREC = lax.Precision.HIGHEST
BETA_ONE = 0.9
BETA_TWO = 0.99
EPSILON = 1e-08
GALORE_SCALE = 0.25
LANES = 128
SUBS = 8


def dot_nn(a, b):
    return lax.dot_general(
        a, b, (((1,), (0,)), ((), ())), precision=HIGHEST_PREC, preferred_element_type=jnp.float32
    )


def dot_nt(a, b):
    return lax.dot_general(
        a, b, (((1,), (1,)), ((), ())), precision=HIGHEST_PREC, preferred_element_type=jnp.float32
    )


def chol_inverse_tile(block):
    width = block.shape[1]
    rows = [block[i * SUBS : (i + 1) * SUBS, :] for i in range(width // SUBS)]
    lane = lax.broadcasted_iota(jnp.int32, (SUBS, width), 1)
    sub = lax.broadcasted_iota(jnp.int32, (SUBS, width), 0)
    full = (SUBS, width)
    done = []
    for j in range(len(rows)):
        base = j * SUBS
        now = rows[j]
        in_block = (lane >= base) & (lane < base + SUBS)
        cols = [
            jnp.broadcast_to(now[:, base + p : base + p + 1], full) for p in range(SUBS)
        ]
        now = jnp.where(in_block, jnp.where(lane - base == sub, 1.0, 0.0), now)
        out = jnp.zeros(full, jnp.float32)
        for p in range(SUBS):
            pivot = jnp.broadcast_to(cols[p][p : p + 1, :], full)
            root = lax.rsqrt(pivot)
            inverse = root * root
            scaled = cols[p] * inverse
            line = jnp.broadcast_to(now[p : p + 1, :], full)
            out = jnp.where(sub == p, line * root, out)
            now = jnp.where(sub == p, line * inverse, now - scaled * line)
            for q in range(p + 1, SUBS):
                head = jnp.broadcast_to(cols[q][p : p + 1, :], full)
                cols[q] = jnp.where(sub == p, head * inverse, cols[q] - scaled * head)
        lines = [jnp.broadcast_to(now[p : p + 1, :], full) for p in range(SUBS)]
        for i in range(j + 1, len(rows)):
            terms = [
                jnp.broadcast_to(rows[i][:, base + p : base + p + 1], full) * lines[p]
                for p in range(SUBS)
            ]
            while len(terms) > 1:
                terms = [terms[k] + terms[k + 1] for k in range(0, len(terms), 2)]
            rows[i] = jnp.where(in_block, 0.0, rows[i]) - terms[0]
        done.append(jnp.where(lane <= base + sub, out, 0.0))
    return jnp.concatenate(done, axis=0)


def chol_inverse(gram_ref, out_ref):
    half = LANES
    first = chol_inverse_tile(gram_ref[:half, :half])
    out_ref[:half, :half] = first
    out_ref[:half, half:] = jnp.zeros((half, half), jnp.float32)
    low = dot_nt(gram_ref[half:, :half], first)
    second = chol_inverse_tile(gram_ref[half:, half:] - dot_nt(low, low))
    out_ref[half:, half:] = second
    out_ref[half:, :half] = -dot_nn(second, dot_nn(low, first))


def refine_kernel(count_ref, square_ref, start_ref, head_ref, state_ref, wide_ref, gram_ref, inv_ref):
    state_ref[...] = start_ref[...]
    head_ref[...] = jnp.zeros_like(head_ref)

    def step(_, carry):
        wide_ref[...] = dot_nn(state_ref[...], square_ref[...])
        gram_ref[...] = dot_nt(state_ref[...], wide_ref[...])
        chol_inverse(gram_ref, inv_ref)
        head_ref[...] = dot_nn(inv_ref[...], state_ref[...])
        state_ref[...] = dot_nn(inv_ref[...], wide_ref[...])
        return carry

    lax.fori_loop(0, count_ref[0], step, 0)


def refine(count, square, start):
    rank, cols = start.shape
    vmem = pl.BlockSpec(memory_space=pltpu.VMEM)
    shape = jax.ShapeDtypeStruct((rank, cols), jnp.float32)
    return pl.pallas_call(
        refine_kernel,
        out_shape=(shape, shape),
        in_specs=[pl.BlockSpec(memory_space=pltpu.SMEM), vmem, vmem],
        out_specs=(vmem, vmem),
        scratch_shapes=[
            pltpu.VMEM((rank, cols), jnp.float32),
            pltpu.VMEM((rank, rank), jnp.float32),
            pltpu.VMEM((rank, rank), jnp.float32),
        ],
        cost_estimate=pl.CostEstimate(
            flops=10 * rank * cols * cols, bytes_accessed=4 * cols * (cols + 3 * rank), transcendentals=0
        ),
        name="refine",
    )(count, square, start)


def pick(stack, index):
    return lax.dynamic_index_in_dim(stack, index, 0, keepdims=False)


def shard_shift(block_of, shift):
    size = lax.axis_size("shard")
    me = lax.axis_index("shard")
    block = block_of(lax.rem(me + shift, size))
    if shift == 0:
        return block
    return lax.ppermute(block, "shard", [(s, (s + shift) % size) for s in range(size)])


def shard_exchange(block_of):
    size = lax.axis_size("shard")
    me = lax.axis_index("shard")
    arrived = [shard_shift(block_of, shift) for shift in range(size)]
    stack = jnp.zeros((size,) + arrived[0].shape, arrived[0].dtype)
    for shift in range(size):
        stack = lax.dynamic_update_index_in_dim(
            stack, arrived[shift], lax.rem(me - shift + size, size), 0
        )
    return stack


def owner_exchange(stack):
    return lax.all_to_all(stack, "owner", split_axis=0, concat_axis=0, tiled=True)


def on_device(gradient, old_basis, moment_one, moment_two, slot_expert, cost):
    slots, rows, cols = gradient.shape
    rank = old_basis.shape[2]
    owners = lax.axis_size("owner")
    owner_now = lax.axis_index("owner")
    shard_now = lax.axis_index("shard")
    table = slot_expert.reshape(owners, slots)
    mine = lax.dynamic_index_in_dim(table, owner_now, 0, keepdims=False)
    home_of = mine // slots
    group = jnp.arange(owners)
    place = jnp.arange(slots)
    slot_for = jnp.sum(jnp.where(home_of[None, :] == group[:, None], place[None, :], 0), axis=1)
    hits = table[:, :, None] == (owner_now * slots + place)[None, None, :]
    local_for = jnp.sum(jnp.where(jnp.any(hits, axis=1), place[None, :], 0), axis=1)
    holder_of = jnp.sum(jnp.where(jnp.any(hits, axis=1), group[:, None], 0), axis=0)
    count = lax.dynamic_slice_in_dim(cost, owner_now * slots + shard_now, 1)

    outgoing = jnp.stack([pick(old_basis, slot_for[h]) for h in range(owners)])
    grad_now = shard_exchange(lambda i: pick(gradient, i)).reshape(-1, cols)
    arrived = owner_exchange(outgoing)
    basis_now = shard_exchange(lambda i: pick(arrived, pick(holder_of, i))).reshape(-1, rank)

    square = jnp.dot(grad_now.T, grad_now, precision=HIGHEST_PREC)
    start = jnp.dot(basis_now.T, grad_now, precision=HIGHEST_PREC)
    head, projected = refine(count, square, start)
    refreshed = lax.dot_general(
        grad_now, head, (((1,), (1,)), ((), ())), precision=HIGHEST_PREC
    )
    basis_new = jnp.where(count[0] > 0, refreshed, basis_now)

    part = projected.reshape(slots, -1, cols)
    proj_home = shard_exchange(lambda i: pick(part, i))
    proj_recv = owner_exchange(jnp.stack([pick(proj_home, local_for[o]) for o in range(owners)]))
    proj_slot = jnp.stack([pick(proj_recv, home_of[j]) for j in range(slots)])
    moment_new = BETA_ONE * moment_one + (1.0 - BETA_ONE) * proj_slot
    second_new = BETA_TWO * moment_two + (1.0 - BETA_TWO) * proj_slot * proj_slot
    normed = moment_new / (jnp.sqrt(second_new) + EPSILON)
    normed_all = lax.all_gather(normed, "shard", axis=1, tiled=True)

    block = basis_new.reshape(slots, rows, rank)
    basis_home = shard_exchange(lambda i: pick(block, i))
    basis_recv = owner_exchange(jnp.stack([pick(basis_home, local_for[o]) for o in range(owners)]))
    basis_slot = jnp.stack([pick(basis_recv, home_of[j]) for j in range(slots)])

    expanded = jnp.einsum("krq,kqc->krc", basis_slot, normed_all, precision=HIGHEST_PREC)
    update = (GALORE_SCALE * expanded).astype(jnp.bfloat16)
    return (basis_slot, moment_new, second_new, update)


def solution(mesh):
    spec = P("owner", "shard", None)
    return jax.shard_map(
        on_device,
        mesh=mesh,
        in_specs=(spec, spec, spec, spec, P(), P()),
        out_specs=(spec, spec, spec, spec),
        check_vma=False,
    )
```

time: 922 us -> 450 us (0.49)
  other arithmetic: 270 us -> 2 us
  matrix products: 200 us -> 45.8 us
  waiting for transfers between devices: 303 us -> 179 us
  starting transfers between devices: 46.6 us -> 111 us
  between operations: 14.5 us -> 61 us
  blocking collectives: 28.9 us -> 0 us
  loops' own time: 11.9 us -> 0 us
    another operation x50 -> x1, other arithmetic: 269 us -> 0.14 us  [on_device(): basis_slot = jnp.stack([pick(basis_recv, home_of[j]) for j in range(slots)])]
    all_to_all x6 -> x3, waiting for transfers between devices: 303 us -> 96.8 us  [owner_exchange(): lax.all_to_all(stack, 'owner', split_axis=0, concat_axis=0, tiled=True)]
    dot_general x23 -> x4, matrix products: 182 us -> 45.8 us  [the longest x1 20.1 us: on_device(): square = jnp.dot(grad_now.T, grad_now, precision=HIGHEST_PREC)]
    ppermute x0 -> x12, waiting for transfers between devices: none -> 82 us  [shard_shift(): lax.ppermute(block, 'shard', [(s, (s + shift) % size) for s in range(size)])]
    all_to_all x6 -> x3, starting transfers between devices: 46.3 us -> 82.8 us  [owner_exchange(): lax.all_to_all(stack, 'owner', split_axis=0, concat_axis=0, tiled=True)]
    all_to_all x1 -> x0, blocking collectives: 28.9 us -> none  [refresh_project(): lax.all_to_all(basis_slices, 'shard', split_axis=0, concat_axis=1, tiled=...]
    ppermute x0 -> x12, starting transfers between devices: none -> 27.8 us  [shard_shift(): lax.ppermute(block, 'shard', [(s, (s + shift) % size) for s in range(size)])]
    another operation x25 -> x0, matrix products: 18.4 us -> none  [the longest x15 16.1 us: whole_step(): lax.linalg.triangular_solve(factor, tall_block, left_side=False, lower=Tr...]
  transfers between devices with their start and end apart: 7 -> 16, of which waited for: 6 -> 9; matrix products, arithmetic and copies ran while one was open for 4% -> 12% of each run, Pallas kernels for 0% -> 0%
where the time goes in v1:
time: 450 us; the launch traced here: 449 us
  waiting for transfers between devices  179 us (40%)
  starting transfers between devices  111 us (25%)
  between operations  61 us (14%)
  local copies, waits for them, and re-layouts  46.8 us (10%)
  matrix products  45.8 us (10%)
    all_to_all x3, waiting for transfers between devices, owner_exchange(): lax.all_to_all(stack, 'owner', split_axis=0, concat_axis=0, tiled=True)  96.8 us
    all_to_all x3, starting transfers between devices, owner_exchange(): lax.all_to_all(stack, 'owner', split_axis=0, concat_axis=0, tiled=True)  82.8 us
    ppermute x12, waiting for transfers between devices, shard_shift(): lax.ppermute(block, 'shard', [(s, (s + shift) % size) for s in range(size)])  82 us
    ppermute x12, starting transfers between devices, shard_shift(): lax.ppermute(block, 'shard', [(s, (s + shift) % size) for s in range(size)])  27.8 us
    dot_general x1, matrix products, on_device(): square = jnp.dot(grad_now.T, grad_now, precision=HIGHEST_PREC)  20.1 us
    unnamed x31, local copies, waits for them, and re-layouts  18.7 us
    dot_general x1, matrix products, on_device(): jnp.einsum('krq,kqc->krc', basis_slot, normed_all, precision=HIGHEST_PREC)  9.91 us
    squeeze x4, local copies, waits for them, and re-layouts, pick(): return lax.dynamic_index_in_dim(stack, index, 0, keepdims=False)  9.46 us
  transfers between devices with their start and end apart: 16, of which 9 were waited for; matrix products, arithmetic and copies ran while one was open for 12% of the time, Pallas kernels for 0%

profile of v1, /device:TPU:0, one launch (start us, length us, event | category | flops | bytes accessed | tf_op | source)
XLA Modules:
  0.0 449.0 jit_solution(304670207336701000)
XLA Ops:
  20.1 1.9 dynamic-slice_dynamic-update-slice_fusion.18
  22.6 1.9 dynamic-slice_dynamic-update-slice_fusion.17
  33.6 7.3 %all-to-all-start = ((f32[8,512,256]{2,1,0:T(8,128)}), f32[8,512,256]{2,1,0:T(8,128)}, u32[]{:S(2)}, u32[]{:S(2)}) async-start(f32[8,512,256]{2,1,0:T(8,128)} %dynamic-slice_dynamic-update-slice_fusion.11), calls=%async_computation | async-start | bytes 8388608 | tf_op jit(solution)/shard_map/all_to_all | solution.py:144
  40.9 3.2 broadcast_in_dim.81
  44.1 5.7 %dynamic-slice_bitcast_fusion = (f32[512,768]{1,0:T(8,128)}, f32[512,768]{1,0:T(8,128)}, f32[4,512,768]{2,1,0:T(8,128)}, f32[512,768]{1,0:T(8,128)}) fusion(f32[4,512,768]{2,1,0:T(8,128)} %param.6, s32[]{:T(128)S(6)} %select_n.174, s32[]{:T(128)S(6)} %select_n.173, f32[4,512,768]{2,1,0:T(8,128)} %broadcast_in_dim.81, s32[]{:T(128)S(6)} %select_n.172, ...), kind=kLoop, calls=%fused_computation.7 | loop fusion | bytes 12582932 | tf_op jit(solution)/shard_map/jit(dynamic_index_in_dim)/squeeze | solution.py:119
  49.8 1.5 collective-permute-start.1
  51.2 1.5 collective-permute-start.2
  61.7 24.5 %collective-permute-done = f32[512,768]{1,0:T(8,128)} collective-permute-done((f32[512,768]{1,0:T(8,128)}, f32[512,768]{1,0:T(8,128)}, u32[]{:S(2)}, u32[]{:S(2)}) %collective-permute-start) | collective-permute-done | bytes 1572896 | tf_op jit(solution)/shard_map/ppermute | solution.py:128
  86.2 2.7 bitcast_dynamic-update-slice_fusion.2
  90.2 29.3 %collective-permute-done.2 = f32[512,768]{1,0:T(8,128)S(1)} collective-permute-done((f32[512,768]{1,0:T(8,128)}, f32[512,768]{1,0:T(8,128)S(1)}, u32[]{:S(2)}, u32[]{:S(2)}) %collective-permute-start.2) | collective-permute-done | bytes 1572896 | tf_op jit(solution)/shard_map/ppermute | solution.py:128
  120.7 13.4 %all-to-all-done = f32[8,512,256]{2,1,0:T(8,128)} async-done(((f32[8,512,256]{2,1,0:T(8,128)}), f32[8,512,256]{2,1,0:T(8,128)}, u32[]{:S(2)}, u32[]{:S(2)}) %all-to-all-start) | async-done | bytes 4194336 | tf_op jit(solution)/shard_map/all_to_all | solution.py:144
  134.3 1.7 dynamic-slice_bitcast_fusion.6
  136.1 1.6 collective-permute-start.4
  137.6 1.4 collective-permute-start.5
  139.0 20.1 %convolution_bitcast_fusion.square_ref = f32[768,768]{1,0:T(8,128)} fusion(f32[4,512,768]{2,1,0:T(8,128)} %bitcast_dynamic-update-slice_fusion), kind=kOutput, calls=%fused_computation.3 | convolution fusion | flops 14495514624 | bytes 8650752 | tf_op jit(solution)/shard_map/dot_general | solution.py:169
  159.2 1.4 collective-permute-done.5
  160.6 8.4 %convolution_bitcast_fusion.1.start_ref = f32[256,768]{1,0:T(8,128)} fusion(f32[4,512,256]{2,1,0:T(8,128)S(1)} %bitcast_dynamic-update-slice_fusion.6, f32[4,512,768]{2,1,0:T(8,128)} %bitcast_dynamic-update-slice_fusion), kind=kOutput, calls=%fused_computation.11 | convolution fusion | flops 4831838208 | bytes 9175040 | tf_op jit(solution)/shard_map/dot_general | solution.py:170
  169.0 4.0 refine.1
  173.0 2.0 dynamic-slice_bitcast_fusion.9
  175.0 17.3 %collective-permute-start.9 = (f32[64,768]{1,0:T(8,128)}, f32[64,768]{1,0:T(8,128)S(1)}, u32[]{:S(2)}, u32[]{:S(2)}) collective-permute-start(f32[64,768]{1,0:T(8,128)} %get-tuple-element.35), channel_id=1, source_target_pairs={{0,8},{8,16},{16,24},{24,0},{1,9},{9,17},{17,25},{25,1},{2,10},{10... | collective-permute-start | bytes 589832 | tf_op jit(solution)/shard_map/ppermute | solution.py:128
  210.0 5.4 %collective-permute-done.10 = f32[64,768]{1,0:T(8,128)S(1)} collective-permute-done((f32[64,768]{1,0:T(8,128)S(1)}, f32[64,768]{1,0:T(8,128)S(1)}, u32[]{:S(2)}, u32[]{:S(2)}) %collective-permute-start.10) | collective-permute-done | bytes 196640 | tf_op jit(solution)/shard_map/ppermute | solution.py:128
  221.0 69.5 %all-to-all-start.2 = ((f32[8,64,768]{2,1,0:T(8,128)}), f32[8,64,768]{2,1,0:T(8,128)}, u32[]{:S(2)}, u32[]{:S(2)}) async-start(f32[8,64,768]{2,1,0:T(8,128)} %dynamic-slice_dynamic-update-slice_fusion.19), calls=%async_computation.2 | async-start | bytes 3145728 | tf_op jit(solution)/shard_map/all_to_all | solution.py:144
  290.5 7.4 %convolution_select_fusion = f32[2048,256]{1,0:T(8,128)S(1)} fusion(f32[2048,256]{1,0:T(8,128)S(1)} %bitcast.99, f32[2048,768]{1,0:T(8,128)} %bitcast.7, f32[256,768]{1,0:T(8,128)} %get-tuple-element.6, pred[]{:T(512)} %bitcast), kind=kOutput, calls=%fused_computation.1 | convolution fusion | flops 4832362496 | bytes 11272193 | tf_op jit(solution)/shard_map/dot_general | solution.py:172
  298.2 1.7 collective-permute-start.6
  301.4 9.0 %collective-permute-done.6 = f32[512,256]{1,0:T(8,128)S(1)} collective-permute-done((f32[512,256]{1,0:T(8,128)S(1)}, f32[512,256]{1,0:T(8,128)S(1)}, u32[]{:S(2)}, u32[]{:S(2)}) %collective-permute-start.6) | collective-permute-done | bytes 524320 | tf_op jit(solution)/shard_map/ppermute | solution.py:128
  310.4 4.3 collective-permute-done.7
  314.7 8.1 %collective-permute-done.8 = f32[512,256]{1,0:T(8,128)S(1)} collective-permute-done((f32[512,256]{1,0:T(8,128)S(1)}, f32[512,256]{1,0:T(8,128)S(1)}, u32[]{:S(2)}, u32[]{:S(2)}) %collective-permute-start.8) | collective-permute-done | bytes 524320 | tf_op jit(solution)/shard_map/ppermute | solution.py:128
  329.6 6.0 %all-to-all-start.1 = ((f32[8,512,256]{2,1,0:T(8,128)}), f32[8,512,256]{2,1,0:T(8,128)}, u32[]{:S(2)}, u32[]{:S(2)}) async-start(f32[8,512,256]{2,1,0:T(8,128)} %dynamic-slice_dynamic-update-slice_fusion.1), calls=%async_computation.1 | async-start | bytes 8388608 | tf_op jit(solution)/shard_map/all_to_all | solution.py:144
  345.4 1.6 add_divide_fusion
  347.0 83.3 %all-to-all-done.1 = f32[8,512,256]{2,1,0:T(8,128)} async-done(((f32[8,512,256]{2,1,0:T(8,128)}), f32[8,512,256]{2,1,0:T(8,128)}, u32[]{:S(2)}, u32[]{:S(2)}) %all-to-all-start.1) | async-done | bytes 4194336 | tf_op jit(solution)/shard_map/all_to_all | solution.py:144
  430.4 1.7 constant_dynamic-slice_fusion.4
  432.2 9.9 %multiply_convert_fusion = bf16[4,512,768]{2,1,0:T(8,128)(2,1)} fusion(f32[4,512,256]{2,1,0:T(8,128)S(1)} %pad_maximum_fusion, f32[4,256,768]{2,1,0:T(8,128)} %all-gather.2.cloned.1.call-done), kind=kOutput, calls=%fused_computation | convolution fusion | flops 4834983936 | bytes 8388608 | tf_op jit(solution)/shard_map/krq,kqc->krc/dot_general | solution.py:191
  (76 shorter events, 29.6 us)
Async XLA Ops:
  7.2 18.0 %copy-start.1 = (f32[4,512,256]{2,1,0:T(8,128)S(1)}, f32[4,512,256]{2,1,0:T(8,128)}, u32[]{:S(2)}) copy-start(f32[4,512,256]{2,1,0:T(8,128)} %param.7) | copy-start | bytes 6291460
  33.6 100.6 %all-to-all-start = ((f32[8,512,256]{2,1,0:T(8,128)}), f32[8,512,256]{2,1,0:T(8,128)}, u32[]{:S(2)}, u32[]{:S(2)}) async-start(f32[8,512,256]{2,1,0:T(8,128)} %dynamic-slice_dynamic-update-slice_fusion.11), calls=%async_computation | async-start | bytes 8388608 | tf_op jit(solution)/shard_map/all_to_all | solution.py:144
  44.1 17.0 %copy-start.4 = (s32[32]{0:T(128)S(1)}, s32[32]{0:T(128)}, u32[]{:S(2)}) copy-start(s32[32]{0:T(128)} %param.11) | copy-start | bytes 388
  49.7 36.4 %collective-permute-start = (f32[512,768]{1,0:T(8,128)}, f32[512,768]{1,0:T(8,128)}, u32[]{:S(2)}, u32[]{:S(2)}) collective-permute-start(f32[512,768]{1,0:T(8,128)} %get-tuple-element.14), channel_id=1, source_target_pairs={{0,8},{8,16},{16,24},{24,0},{1,9},{9,17},{17,25},{25,1},{2,10},{10... | collective-permute-start | bytes 4718600 | tf_op jit(solution)/shard_map/ppermute | solution.py:128
  49.8 39.1 %collective-permute-start.1 = (f32[512,768]{1,0:T(8,128)}, f32[512,768]{1,0:T(8,128)S(1)}, u32[]{:S(2)}, u32[]{:S(2)}) collective-permute-start(f32[512,768]{1,0:T(8,128)} %get-tuple-element.16), channel_id=1, source_target_pairs={{0,16},{8,24},{16,0},{24,8},{1,17},{9,25},{17,1},{25,9},{2,18},{10... | collective-permute-start | bytes 4718600 | tf_op jit(solution)/shard_map/ppermute | solution.py:128
  51.2 68.2 %collective-permute-start.2 = (f32[512,768]{1,0:T(8,128)}, f32[512,768]{1,0:T(8,128)S(1)}, u32[]{:S(2)}, u32[]{:S(2)}) collective-permute-start(f32[512,768]{1,0:T(8,128)} %get-tuple-element.13), channel_id=1, source_target_pairs={{0,24},{8,0},{16,8},{24,16},{1,25},{9,1},{17,9},{25,17},{2,26},{10... | collective-permute-start | bytes 4718600 | tf_op jit(solution)/shard_map/ppermute | solution.py:128
  136.0 23.1 %collective-permute-start.3 = (f32[512,256]{1,0:T(8,128)S(1)}, f32[512,256]{1,0:T(8,128)S(1)}, u32[]{:S(2)}, u32[]{:S(2)}) collective-permute-start(f32[512,256]{1,0:T(8,128)S(1)} %get-tuple-element.23), channel_id=1, source_target_pairs={{0,8},{8,16},{16,24},{24,0},{1,9},{9,17},{17,25},{25,1},{2,10},{10... | collective-permute-start | bytes 1572872 | tf_op jit(solution)/shard_map/ppermute | solution.py:128
  136.1 23.0 %collective-permute-start.4 = (f32[512,256]{1,0:T(8,128)S(1)}, f32[512,256]{1,0:T(8,128)S(1)}, u32[]{:S(2)}, u32[]{:S(2)}) collective-permute-start(f32[512,256]{1,0:T(8,128)S(1)} %get-tuple-element.22), channel_id=1, source_target_pairs={{0,16},{8,24},{16,0},{24,8},{1,17},{9,25},{17,1},{25,9},{2,18},{10... | collective-permute-start | bytes 1572872 | tf_op jit(solution)/shard_map/ppermute | solution.py:128
  137.6 22.9 %collective-permute-start.5 = (f32[512,256]{1,0:T(8,128)S(1)}, f32[512,256]{1,0:T(8,128)S(1)}, u32[]{:S(2)}, u32[]{:S(2)}) collective-permute-start(f32[512,256]{1,0:T(8,128)S(1)} %get-tuple-element.21), channel_id=1, source_target_pairs={{0,24},{8,0},{16,8},{24,16},{1,25},{9,1},{17,9},{25,17},{2,26},{10... | collective-permute-start | bytes 1572872 | tf_op jit(solution)/shard_map/ppermute | solution.py:128
  175.0 35.0 %collective-permute-start.9 = (f32[64,768]{1,0:T(8,128)}, f32[64,768]{1,0:T(8,128)S(1)}, u32[]{:S(2)}, u32[]{:S(2)}) collective-permute-start(f32[64,768]{1,0:T(8,128)} %get-tuple-element.35), channel_id=1, source_target_pairs={{0,8},{8,16},{16,24},{24,0},{1,9},{9,17},{17,25},{25,1},{2,10},{10... | collective-permute-start | bytes 589832 | tf_op jit(solution)/shard_map/ppermute | solution.py:128
  208.6 6.9 %collective-permute-start.10 = (f32[64,768]{1,0:T(8,128)S(1)}, f32[64,768]{1,0:T(8,128)S(1)}, u32[]{:S(2)}, u32[]{:S(2)}) collective-permute-start(f32[64,768]{1,0:T(8,128)S(1)} %get-tuple-element.34), channel_id=1, source_target_pairs={{0,16},{8,24},{16,0},{24,8},{1,17},{9,25},{17,1},{25,9},{2,18},{10... | collective-permute-start | bytes 589832 | tf_op jit(solution)/shard_map/ppermute | solution.py:128
  208.6 6.8 %collective-permute-start.11 = (f32[64,768]{1,0:T(8,128)S(1)}, f32[64,768]{1,0:T(8,128)S(1)}, u32[]{:S(2)}, u32[]{:S(2)}) collective-permute-start(f32[64,768]{1,0:T(8,128)S(1)} %get-tuple-element.33), channel_id=1, source_target_pairs={{0,24},{8,0},{16,8},{24,16},{1,25},{9,1},{17,9},{25,17},{2,26},{10... | collective-permute-start | bytes 589832 | tf_op jit(solution)/shard_map/ppermute | solution.py:128
  221.0 108.6 %all-to-all-start.2 = ((f32[8,64,768]{2,1,0:T(8,128)}), f32[8,64,768]{2,1,0:T(8,128)}, u32[]{:S(2)}, u32[]{:S(2)}) async-start(f32[8,64,768]{2,1,0:T(8,128)} %dynamic-slice_dynamic-update-slice_fusion.19), calls=%async_computation.2 | async-start | bytes 3145728 | tf_op jit(solution)/shard_map/all_to_all | solution.py:144
  298.2 12.1 %collective-permute-start.6 = (f32[512,256]{1,0:T(8,128)S(1)}, f32[512,256]{1,0:T(8,128)S(1)}, u32[]{:S(2)}, u32[]{:S(2)}) collective-permute-start(f32[512,256]{1,0:T(8,128)S(1)} %get-tuple-element.27), channel_id=1, source_target_pairs={{0,8},{8,16},{16,24},{24,0},{1,9},{9,17},{17,25},{25,1},{2,10},{10... | collective-permute-start | bytes 1572872 | tf_op jit(solution)/shard_map/ppermute | solution.py:128
  299.9 14.8 %collective-permute-start.7 = (f32[512,256]{1,0:T(8,128)S(1)}, f32[512,256]{1,0:T(8,128)S(1)}, u32[]{:S(2)}, u32[]{:S(2)}) collective-permute-start(f32[512,256]{1,0:T(8,128)S(1)} %get-tuple-element.26), channel_id=1, source_target_pairs={{0,16},{8,24},{16,0},{24,8},{1,17},{9,25},{17,1},{25,9},{2,18},{10... | collective-permute-start | bytes 1572872 | tf_op jit(solution)/shard_map/ppermute | solution.py:128
  300.2 22.7 %collective-permute-start.8 = (f32[512,256]{1,0:T(8,128)S(1)}, f32[512,256]{1,0:T(8,128)S(1)}, u32[]{:S(2)}, u32[]{:S(2)}) collective-permute-start(f32[512,256]{1,0:T(8,128)S(1)} %get-tuple-element.25), channel_id=1, source_target_pairs={{0,24},{8,0},{16,8},{24,16},{1,25},{9,1},{17,9},{25,17},{2,26},{10... | collective-permute-start | bytes 1572872 | tf_op jit(solution)/shard_map/ppermute | solution.py:128
  329.6 100.7 %all-to-all-start.1 = ((f32[8,512,256]{2,1,0:T(8,128)}), f32[8,512,256]{2,1,0:T(8,128)}, u32[]{:S(2)}, u32[]{:S(2)}) async-start(f32[8,512,256]{2,1,0:T(8,128)} %dynamic-slice_dynamic-update-slice_fusion.1), calls=%async_computation.1 | async-start | bytes 8388608 | tf_op jit(solution)/shard_map/all_to_all | solution.py:144
  335.6 9.7 %copy-start.2 = (f32[4,64,768]{2,1,0:T(8,128)S(1)}, f32[4,64,768]{2,1,0:T(8,128)}, u32[]{:S(2)}) copy-start(f32[4,64,768]{2,1,0:T(8,128)} %param.9) | copy-start | bytes 2359300
  335.6 9.8 %copy-start.3 = (f32[4,64,768]{2,1,0:T(8,128)S(1)}, f32[4,64,768]{2,1,0:T(8,128)}, u32[]{:S(2)}) copy-start(f32[4,64,768]{2,1,0:T(8,128)} %param.8) | copy-start | bytes 2359300
  335.7 96.5 %all-gather.2.cloned.1.call-start = ((), (), s32[]{:S(2)}) async-start(), calls=%async_computation.3 | async-start | bytes 3932160 | tf_op jit(solution)/shard_map/all_gather | solution.py:184
  432.2 10.0 %copy-start = (f32[4,512,256]{2,1,0:T(8,128)}, f32[4,512,256]{2,1,0:T(8,128)S(1)}, u32[]{:S(2)}) copy-start(f32[4,512,256]{2,1,0:T(8,128)S(1)} %pad_maximum_fusion) | copy-start | bytes 6291460
Sparse Core Ops, SparseCore 0:
  347.2 30.1 all-gather.1

commit v2 on v1

v2 whole, which is shorter than its diff:
```python
import functools

import jax
import jax.numpy as jnp
from jax import lax
from jax.experimental import pallas as pl
from jax.experimental.pallas import tpu as pltpu
from jax.sharding import PartitionSpec as P

HIGHEST_PREC = lax.Precision.HIGHEST
HIGH_PREC = lax.Precision.HIGH
BETA_ONE = 0.9
BETA_TWO = 0.99
EPSILON = 1e-08
GALORE_SCALE = 0.25
SUBS = 8


def dot_nn(a, b):
    return lax.dot_general(
        a, b, (((1,), (0,)), ((), ())), precision=HIGHEST_PREC, preferred_element_type=jnp.float32
    )


def dot_nt(a, b):
    return lax.dot_general(
        a, b, (((1,), (1,)), ((), ())), precision=HIGHEST_PREC, preferred_element_type=jnp.float32
    )


def chol_inverse_tile(block):
    width = block.shape[1]
    rows = [block[i * SUBS : (i + 1) * SUBS, :] for i in range(width // SUBS)]
    lane = lax.broadcasted_iota(jnp.int32, (SUBS, width), 1)
    sub = lax.broadcasted_iota(jnp.int32, (SUBS, width), 0)
    full = (SUBS, width)
    done = []
    for j in range(len(rows)):
        base = j * SUBS
        now = rows[j]
        in_block = (lane >= base) & (lane < base + SUBS)
        cols = [
            jnp.where(lane >= 0, jnp.broadcast_to(now[:, base + p : base + p + 1], full), 0.0)
            for p in range(SUBS)
        ]
        now = jnp.where(in_block, jnp.where(lane - base == sub, 1.0, 0.0), now)
        out = jnp.zeros(full, jnp.float32)
        for p in range(SUBS):
            pivot = jnp.broadcast_to(cols[p][p : p + 1, :], full)
            root = lax.rsqrt(pivot)
            inverse = root * root
            scaled = cols[p] * inverse
            line = jnp.broadcast_to(now[p : p + 1, :], full)
            out = jnp.where(sub == p, line * root, out)
            now = jnp.where(sub == p, line * inverse, now - scaled * line)
            for q in range(p + 1, SUBS):
                head = jnp.broadcast_to(cols[q][p : p + 1, :], full)
                cols[q] = jnp.where(sub == p, head * inverse, cols[q] - scaled * head)
        lines = [jnp.broadcast_to(now[p : p + 1, :], full) for p in range(SUBS)]
        for i in range(j + 1, len(rows)):
            terms = [
                jnp.broadcast_to(rows[i][:, base + p : base + p + 1], full) * lines[p]
                for p in range(SUBS)
            ]
            while len(terms) > 1:
                terms = [terms[k] + terms[k + 1] for k in range(0, len(terms), 2)]
            rows[i] = jnp.where(in_block, 0.0, rows[i]) - terms[0]
        done.append(jnp.where(lane <= base + sub, out, 0.0))
    return jnp.concatenate(done, axis=0)


def chol_inverse(gram_ref, out_ref):
    half = gram_ref.shape[0] // 2
    first = chol_inverse_tile(gram_ref[:half, :half])
    out_ref[:half, :half] = first
    out_ref[:half, half:] = jnp.zeros((half, half), jnp.float32)
    low = dot_nt(gram_ref[half:, :half], first)
    second = chol_inverse_tile(gram_ref[half:, half:] - dot_nt(low, low))
    out_ref[half:, half:] = second
    out_ref[half:, :half] = -dot_nn(second, dot_nn(low, first))


def split(x):
    high = x.astype(jnp.bfloat16)
    return high, (x - high.astype(jnp.float32)).astype(jnp.bfloat16)


def dot_split(a, b, contract):
    def one(x, y):
        return lax.dot_general(
            x, y, (contract, ((), ())), preferred_element_type=jnp.float32
        )

    return one(a[0], b[1]) + one(a[1], b[0]) + one(a[0], b[0])


NN = ((1,), (0,))
NT = ((1,), (1,))


def refine_kernel(
    count_ref, square_ref, start_ref, head_ref, state_ref, square_parts, state_parts, wide_parts, gram_ref, inv_ref
):
    count = count_ref[0]
    state_ref[...] = start_ref[...]
    head_ref[...] = jnp.zeros_like(head_ref)
    square_parts[0], square_parts[1] = split(square_ref[...])
    state_parts[0], state_parts[1] = split(start_ref[...])

    def step(index, carry):
        state = (state_parts[0], state_parts[1])
        wide = split(dot_split(state, (square_parts[0], square_parts[1]), NN))
        wide_parts[0], wide_parts[1] = wide
        gram_ref[...] = dot_split(state, wide, NT)
        chol_inverse(gram_ref, inv_ref)
        inverse = split(inv_ref[...])

        @pl.when(index == count - 1)
        def _():
            head_ref[...] = dot_split(inverse, (state_parts[0], state_parts[1]), NN)

        fresh = dot_split(inverse, (wide_parts[0], wide_parts[1]), NN)
        state_ref[...] = fresh
        state_parts[0], state_parts[1] = split(fresh)
        return carry

    lax.fori_loop(0, count, step, 0)


def refine(count, square, start):
    rank, cols = start.shape
    vmem = pl.BlockSpec(memory_space=pltpu.VMEM)
    shape = jax.ShapeDtypeStruct((rank, cols), jnp.float32)
    return pl.pallas_call(
        refine_kernel,
        out_shape=(shape, shape),
        in_specs=[pl.BlockSpec(memory_space=pltpu.SMEM), vmem, vmem],
        out_specs=(vmem, vmem),
        scratch_shapes=[
            pltpu.VMEM((2, cols, cols), jnp.bfloat16),
            pltpu.VMEM((2, rank, cols), jnp.bfloat16),
            pltpu.VMEM((2, rank, cols), jnp.bfloat16),
            pltpu.VMEM((rank, rank), jnp.float32),
            pltpu.VMEM((rank, rank), jnp.float32),
        ],
        cost_estimate=pl.CostEstimate(
            flops=10 * rank * cols * cols, bytes_accessed=4 * cols * (cols + 3 * rank), transcendentals=0
        ),
        name="refine",
    )(count, square, start)


class Places:
    def __init__(self, owners, slots):
        self.owners, self.slots = owners, slots

    def home_of(self, slot, ids, table):
        return lax.div(table[ids[0] * self.slots + slot], self.slots)

    def slot_for(self, home, ids, table):
        found = 0
        for slot in range(self.slots):
            found = jnp.where(self.home_of(slot, ids, table) == home, slot, found)
        return found

    def local_for(self, holder, ids, table):
        found = 0
        for slot in range(self.slots):
            expert = table[holder * self.slots + slot]
            hit = lax.div(expert, self.slots) == ids[0]
            found = jnp.where(hit, lax.rem(expert, self.slots), found)
        return found

    def holder_of(self, local, ids, table):
        wanted = ids[0] * self.slots + local
        found = 0
        for entry in range(self.owners * self.slots):
            found = jnp.where(table[entry] == wanted, entry // self.slots, found)
        return found


def copy_block(ids_ref, table_ref, in_ref, out_ref):
    out_ref[...] = in_ref[...]


def pick_stack(ids, table, stack, number, index):
    block = (1,) + stack.shape[1:]
    return pl.pallas_call(
        copy_block,
        out_shape=jax.ShapeDtypeStruct((number,) + stack.shape[1:], stack.dtype),
        grid_spec=pltpu.PrefetchScalarGridSpec(
            num_scalar_prefetch=2,
            grid=(number,),
            in_specs=[pl.BlockSpec(block, lambda n, i, t: (index(n, i, t), 0, 0))],
            out_specs=pl.BlockSpec(block, lambda n, i, t: (n, 0, 0)),
        ),
        name="pick_stack",
    )(ids, table, stack)


def copy_apart(number, ids_ref, table_ref, *refs):
    for k in range(number):
        refs[number + k][...] = refs[k][0]


def pick_apart(ids, table, stack, number, index, steps=2):
    _, rows, cols = stack.shape
    part = rows // steps

    def source(k):
        return pl.BlockSpec((1, part, cols), lambda r, i, t: (index(k, i, t), r, 0))

    return pl.pallas_call(
        functools.partial(copy_apart, number),
        out_shape=[jax.ShapeDtypeStruct((rows, cols), stack.dtype)] * number,
        grid_spec=pltpu.PrefetchScalarGridSpec(
            num_scalar_prefetch=2,
            grid=(steps,),
            in_specs=[source(k) for k in range(number)],
            out_specs=[pl.BlockSpec((part, cols), lambda r, i, t: (r, 0))] * number,
        ),
        name="pick_apart",
    )(ids, table, *([stack] * number))


def choose_block(places, number, ids_ref, table_ref, *refs):
    out_ref = refs[number]
    for holder in range(places.owners):
        local = places.local_for(holder, ids_ref, table_ref)
        shift = lax.rem(local - ids_ref[1] + number, number)
        for k in range(number):

            @pl.when(shift == k)
            def _():
                out_ref[holder] = refs[k][...]


def stack_for_holders(places, ids, table, blocks, steps):
    rows, cols = blocks[0].shape
    part = rows // steps
    return pl.pallas_call(
        functools.partial(choose_block, places, len(blocks)),
        out_shape=jax.ShapeDtypeStruct((places.owners, rows, cols), blocks[0].dtype),
        grid_spec=pltpu.PrefetchScalarGridSpec(
            num_scalar_prefetch=2,
            grid=(steps,),
            in_specs=[pl.BlockSpec((part, cols), lambda r, i, t: (r, 0))] * len(blocks),
            out_specs=pl.BlockSpec((places.owners, part, cols), lambda r, i, t: (0, r, 0)),
        ),
        name="stack_for_holders",
    )(ids, table, *blocks)


def adam_kernel(ids_ref, table_ref, proj_ref, one_ref, two_ref, one_out, two_out, normed_ref):
    projected = proj_ref[...]
    moment_new = BETA_ONE * one_ref[...] + (1.0 - BETA_ONE) * projected
    second_new = BETA_TWO * two_ref[...] + (1.0 - BETA_TWO) * projected * projected
    one_out[...] = moment_new
    two_out[...] = second_new
    normed_ref[...] = moment_new / (jnp.sqrt(second_new) + EPSILON)


def adam(places, ids, table, received, moment_one, moment_two):
    block = (1,) + moment_one.shape[1:]
    own = pl.BlockSpec(block, lambda n, i, t: (n, 0, 0))
    shape = jax.ShapeDtypeStruct(moment_one.shape, moment_one.dtype)
    return pl.pallas_call(
        adam_kernel,
        out_shape=[shape] * 3,
        grid_spec=pltpu.PrefetchScalarGridSpec(
            num_scalar_prefetch=2,
            grid=(moment_one.shape[0],),
            in_specs=[
                pl.BlockSpec(block, lambda n, i, t: (places.home_of(n, i, t), 0, 0)),
                own,
                own,
            ],
            out_specs=[own] * 3,
        ),
        name="adam",
    )(ids, table, received, moment_one, moment_two)


def update_kernel(ids_ref, table_ref, basis_ref, normed_ref, basis_out, update_ref):
    basis = basis_ref[0]
    basis_out[0] = basis
    expanded = dot_split(split(basis), split(normed_ref[0]), NN)
    update_ref[0] = (GALORE_SCALE * expanded).astype(update_ref.dtype)


def updates(places, ids, table, received, normed, slots):
    _, rows, rank = received.shape
    cols = normed.shape[2]
    return pl.pallas_call(
        update_kernel,
        out_shape=[
            jax.ShapeDtypeStruct((slots, rows, rank), jnp.float32),
            jax.ShapeDtypeStruct((slots, rows, cols), jnp.bfloat16),
        ],
        grid_spec=pltpu.PrefetchScalarGridSpec(
            num_scalar_prefetch=2,
            grid=(slots,),
            in_specs=[
                pl.BlockSpec((1, rows, rank), lambda n, i, t: (places.home_of(n, i, t), 0, 0)),
                pl.BlockSpec((1, rank, cols), lambda n, i, t: (n, 0, 0)),
            ],
            out_specs=[
                pl.BlockSpec((1, rows, rank), lambda n, i, t: (n, 0, 0)),
                pl.BlockSpec((1, rows, cols), lambda n, i, t: (n, 0, 0)),
            ],
        ),
        name="updates",
    )(ids, table, received, normed)


def send(block, shift):
    size = lax.axis_size("shard")
    if shift % size == 0:
        return block
    return lax.ppermute(block, "shard", [(s, (s + shift) % size) for s in range(size)])


def owner_exchange(stack):
    return lax.all_to_all(stack, "owner", split_axis=0, concat_axis=0, tiled=True)


def dot(a, b, contract):
    return lax.dot_general(
        a, b, (contract, ((), ())), precision=HIGH_PREC, preferred_element_type=jnp.float32
    )


TN = ((0,), (0,))


def on_device(gradient, old_basis, moment_one, moment_two, slot_expert, cost):
    slots = gradient.shape[0]
    rank, cols = moment_one.shape[1] * lax.axis_size("shard"), gradient.shape[2]
    owners, size = lax.axis_size("owner"), lax.axis_size("shard")
    owner_now, shard_now = lax.axis_index("owner"), lax.axis_index("shard")
    places = Places(owners, slots)
    ids = jnp.stack([owner_now, shard_now])
    table = slot_expert
    count = lax.dynamic_slice_in_dim(cost, owner_now * slots + shard_now, 1)

    def onward(shift, ids_ref):
        return lax.rem(ids_ref[1] + shift, size)

    outgoing = pick_stack(ids, table, old_basis, owners, places.slot_for)
    arrived = owner_exchange(outgoing)
    grad_out = pick_apart(ids, table, gradient, size, lambda k, i, t: onward(k, i))
    grads = [send(block, k) for k, block in enumerate(grad_out)]
    square = sum(dot(g, g, TN) for g in grads)
    basis_out = pick_apart(
        ids, table, arrived, size, lambda k, i, t: places.holder_of(onward(k, i), i, t)
    )
    bases = [send(block, k) for k, block in enumerate(basis_out)]
    start = sum(dot(b, g, TN) for b, g in zip(bases, grads))

    head, projected = refine(count, square, start)

    proj_rows = rank // size
    proj_out = pick_apart(
        ids,
        table,
        projected.reshape(size, proj_rows, cols),
        size,
        lambda k, i, t: lax.rem(i[1] - k + size, size),
        steps=1,
    )
    proj_home = [send(block, -k) for k, block in enumerate(proj_out)]
    proj_recv = owner_exchange(stack_for_holders(places, ids, table, proj_home, 1))
    moment_new, second_new, normed = adam(places, ids, table, proj_recv, moment_one, moment_two)
    normed_all = lax.all_gather(normed, "shard", axis=1, tiled=True)

    fresh = [jnp.where(count[0] > 0, dot(g, head, NT), b) for g, b in zip(grads, bases)]
    basis_home = [send(block, -k) for k, block in enumerate(fresh)]
    basis_recv = owner_exchange(stack_for_holders(places, ids, table, basis_home, 4))

    basis_slot, update = updates(places, ids, table, basis_recv, normed_all, slots)
    return (basis_slot, moment_new, second_new, update)


def solution(mesh):
    spec = P("owner", "shard", None)
    return jax.shard_map(
        on_device,
        mesh=mesh,
        in_specs=(spec, spec, spec, spec, P(), P()),
        out_specs=(spec, spec, spec, spec),
        check_vma=False,
    )
```

time: 450 us -> 381 us (0.85)
  Pallas kernels: 3.96 us -> 56.2 us
  between operations: 61 us -> 14.9 us
  local copies, waits for them, and re-layouts: 46.8 us -> 3.75 us
  starting transfers between devices: 111 us -> 72.5 us
  waiting for transfers between devices: 179 us -> 197 us
  matrix products: 45.8 us -> 34 us
    pallas_call x0 -> x8, Pallas kernels: none -> 39.9 us  [the longest x3 11.6 us: pick_apart(): pl.pallas_call(functools.partial(copy_apart, number), out_shape=[jax.Shap...]
    all_gather x1, waiting for transfers between devices: 0.02 us -> 31 us  [on_device(): normed_all = lax.all_gather(normed, 'shard', axis=1, tiled=True)]
    all_to_all x3, starting transfers between devices: 82.8 us -> 60.5 us  [owner_exchange(): lax.all_to_all(stack, 'owner', split_axis=0, concat_axis=0, tiled=True)]
    all_to_all x3, waiting for transfers between devices: 96.8 us -> 74.6 us  [owner_exchange(): lax.all_to_all(stack, 'owner', split_axis=0, concat_axis=0, tiled=True)]
    ppermute x12, starting transfers between devices: 27.8 us -> 11.9 us  [send(): lax.ppermute(block, 'shard', [(s, (s + shift) % size) for s in range(size)])]
    unnamed x31 -> x36, local copies, waits for them, and re-layouts: 18.7 us -> 3.12 us
    pallas_call x1, Pallas kernels: 3.96 us -> 16.3 us  [refine(): pl.pallas_call(refine_kernel, out_shape=(shape, shape), in_specs=[pl.Bloc...]
    dot_general x4 -> x12, matrix products: 45.8 us -> 34 us  [dot(): lax.dot_general(a, b, (contract, ((), ())), precision=HIGH_PREC, preferre...]
  transfers between devices with their start and end apart: 16 -> 16, of which waited for: 9 -> 12; matrix products, arithmetic and copies ran while one was open for 12% -> 9% of each run, Pallas kernels for 0% -> 5%
where the time goes in v2:
time: 381 us; the launch traced here: 379 us
  waiting for transfers between devices  197 us (52%)
  starting transfers between devices  72.5 us (19%)
  Pallas kernels  56.2 us (15%)
  matrix products  34 us (9%)
  between operations  14.9 us (4%)
    ppermute x12, waiting for transfers between devices, send(): lax.ppermute(block, 'shard', [(s, (s + shift) % size) for s in range(size)])  91.1 us
    all_to_all x3, waiting for transfers between devices, owner_exchange(): lax.all_to_all(stack, 'owner', split_axis=0, concat_axis=0, tiled=True)  74.6 us
    all_to_all x3, starting transfers between devices, owner_exchange(): lax.all_to_all(stack, 'owner', split_axis=0, concat_axis=0, tiled=True)  60.5 us
    dot_general x12, matrix products, dot(): lax.dot_general(a, b, (contract, ((), ())), precision=HIGH_PREC, preferre...  34 us
    all_gather x1, waiting for transfers between devices, on_device(): normed_all = lax.all_gather(normed, 'shard', axis=1, tiled=True)  31 us
    pallas_call x1, Pallas kernels, refine(): pl.pallas_call(refine_kernel, out_shape=(shape, shape), in_specs=[pl.Bloc...  16.3 us
    ppermute x12, starting transfers between devices, send(): lax.ppermute(block, 'shard', [(s, (s + shift) % size) for s in range(size)])  11.9 us
    pallas_call x3, Pallas kernels, pick_apart(): pl.pallas_call(functools.partial(copy_apart, number), out_shape=[jax.Shap...  11.6 us
  transfers between devices with their start and end apart: 16, of which 12 were waited for; matrix products, arithmetic and copies ran while one was open for 9% of the time, Pallas kernels for 5%

profile of v2, /device:TPU:0, one launch (start us, length us, event | category | flops | bytes accessed | tf_op | source)
XLA Modules:
  0.0 378.7 jit_solution(1674780059215863532)
XLA Ops:
  7.8 7.3 %pick_stack.1 = f32[8,512,256]{2,1,0:T(8,128)} custom-call(s32[2]{0:T(128)} %pad_add_fusion.ids_ref, s32[32]{0:T(128)} %table_ref.15, f32[4,512,256]{2,1,0:T(8,128)} %in_ref.1), custom_call_target="tpu_custom_call" | custom-call | tf_op jit(solution)/shard_map/pick_stack/pallas_call | solution.py:188
  15.1 7.5 %all-to-all-start = ((f32[8,512,256]{2,1,0:T(8,128)}), f32[8,512,256]{2,1,0:T(8,128)}, u32[]{:S(2)}, u32[]{:S(2)}) async-start(f32[8,512,256]{2,1,0:T(8,128)} %pick_stack.1), calls=%async_computation | async-start | bytes 8388608 | tf_op jit(solution)/shard_map/all_to_all | solution.py:324
  22.6 5.5 %pick_apart.3 = (f32[512,768]{1,0:T(8,128)}, f32[512,768]{1,0:T(8,128)}, f32[512,768]{1,0:T(8,128)}, f32[512,768]{1,0:T(8,128)}) custom-call(s32[2]{0:T(128)} %pad_add_fusion.ids_ref, s32[32]{0:T(128)} %table_ref.15, f32[4,512,768]{2,1,0:T(8,128)} %refs_3_.1, f32[4,512,768]{2,1,0:T(8,128)} %refs_3_.1, f32[4,512,768]{2,1,0:T(8,128)} %refs_3_.1, ...), custom_call_target="tpu_custom_call" | custom-call | tf_op jit(solution)/shard_map/pick_apart/pallas_call | solution.py:213
  29.6 1.7 collective-permute-start.2
  31.9 5.6 %fusion.1 = f32[768,768]{1,0:T(8,128)} fusion(f32[512,768]{1,0:T(8,128)} %get-tuple-element.23), kind=kOutput, calls=%fused_computation.9 | convolution fusion | flops 1811939328 | bytes 3932160 | tf_op jit(solution)/shard_map/dot_general | solution.py:328
  37.5 28.0 %collective-permute-done.1 = f32[512,768]{1,0:T(8,128)S(1)} collective-permute-done((f32[512,768]{1,0:T(8,128)}, f32[512,768]{1,0:T(8,128)S(1)}, u32[]{:S(2)}, u32[]{:S(2)}) %collective-permute-start.1) | collective-permute-done | bytes 1572896 | tf_op jit(solution)/shard_map/ppermute | solution.py:320
  65.5 3.6 fusion.3
  69.2 27.2 %collective-permute-done = f32[512,768]{1,0:T(8,128)S(1)} collective-permute-done((f32[512,768]{1,0:T(8,128)}, f32[512,768]{1,0:T(8,128)S(1)}, u32[]{:S(2)}, u32[]{:S(2)}) %collective-permute-start) | collective-permute-done | bytes 1572896 | tf_op jit(solution)/shard_map/ppermute | solution.py:320
  96.4 3.8 fusion.2
  100.2 15.7 %all-to-all-done.refs_0_.refs_1_.refs_2_.refs_3_ = f32[8,512,256]{2,1,0:T(8,128)} async-done(((f32[8,512,256]{2,1,0:T(8,128)}), f32[8,512,256]{2,1,0:T(8,128)}, u32[]{:S(2)}, u32[]{:S(2)}) %all-to-all-start) | async-done | bytes 4194336 | tf_op jit(solution)/shard_map/all_to_all | solution.py:324
  115.9 3.4 pick_apart.4
  119.4 8.0 %add_add_fusion.square_ref = f32[768,768]{1,0:T(8,128)} fusion(f32[768,768]{1,0:T(8,128)} %fusion.3, f32[768,768]{1,0:T(8,128)} %fusion.1, f32[768,768]{1,0:T(8,128)} %fusion.2, f32[512,768]{1,0:T(8,128)} %collective-permute-done.2), kind=kOutput, calls=%fused_computation | convolution fusion | flops 1813708800 | bytes 11010048 | tf_op jit(solution)/shard_map/dot_general | solution.py:328
  130.2 2.5 fusion.5
  132.7 8.0 %collective-permute-done.3 = f32[512,256]{1,0:T(8,128)S(1)} collective-permute-done((f32[512,256]{1,0:T(8,128)S(1)}, f32[512,256]{1,0:T(8,128)S(1)}, u32[]{:S(2)}, u32[]{:S(2)}) %collective-permute-start.3) | collective-permute-done | bytes 524320 | tf_op jit(solution)/shard_map/ppermute | solution.py:320
  143.3 1.8 fusion.start_ref
  145.1 16.3 %refine.1 = (f32[256,768]{1,0:T(8,128)}, f32[256,768]{1,0:T(8,128)}) custom-call(s32[1]{0:T(128)} %dynamic_slice.3.count_ref, f32[768,768]{1,0:T(8,128)} %add_add_fusion.square_ref, f32[256,768]{1,0:T(8,128)} %fusion.start_ref), custom_call_target="tpu_custom_call" | custom-call | flops 1509949440 | bytes 4718592 | tf_op jit(solution)/shard_map/refine/pallas_call | solution.py:134
  161.4 2.8 pick_apart.5
  164.1 5.6 %collective-permute-start.9 = (f32[64,768]{1,0:T(8,128)}, f32[64,768]{1,0:T(8,128)S(1)}, u32[]{:S(2)}, u32[]{:S(2)}) collective-permute-start(f32[64,768]{1,0:T(8,128)} %get-tuple-element.34), channel_id=1, source_target_pairs={{0,24},{8,0},{16,8},{24,16},{1,25},{9,1},{17,9},{25,17},{2,26},{10... | collective-permute-start | bytes 589832 | tf_op jit(solution)/shard_map/ppermute | solution.py:320
  170.3 5.1 %collective-permute-done.9.refs_1_ = f32[64,768]{1,0:T(8,128)S(1)} collective-permute-done((f32[64,768]{1,0:T(8,128)}, f32[64,768]{1,0:T(8,128)S(1)}, u32[]{:S(2)}, u32[]{:S(2)}) %collective-permute-start.9) | collective-permute-done | bytes 196640 | tf_op jit(solution)/shard_map/ppermute | solution.py:320
  175.4 4.5 %collective-permute-done.10.refs_2_ = f32[64,768]{1,0:T(8,128)S(1)} collective-permute-done((f32[64,768]{1,0:T(8,128)}, f32[64,768]{1,0:T(8,128)S(1)}, u32[]{:S(2)}, u32[]{:S(2)}) %collective-permute-start.10) | collective-permute-done | bytes 196640 | tf_op jit(solution)/shard_map/ppermute | solution.py:320
  180.6 3.6 stack_for_holders.3
  184.2 48.2 %all-to-all-start.2 = ((f32[8,64,768]{2,1,0:T(8,128)}), f32[8,64,768]{2,1,0:T(8,128)}, u32[]{:S(2)}, u32[]{:S(2)}) async-start(f32[8,64,768]{2,1,0:T(8,128)} %stack_for_holders.3), calls=%async_computation.2 | async-start | bytes 3145728 | tf_op jit(solution)/shard_map/all_to_all | solution.py:324
  233.0 2.1 convolution_select_fusion.2
  236.1 2.4 convolution_select_fusion
  240.6 6.1 %collective-permute-done.6.refs_1_ = f32[512,256]{1,0:T(8,128)S(1)} collective-permute-done((f32[512,256]{1,0:T(8,128)S(1)}, f32[512,256]{1,0:T(8,128)S(1)}, u32[]{:S(2)}, u32[]{:S(2)}) %collective-permute-start.6) | collective-permute-done | bytes 524320 | tf_op jit(solution)/shard_map/ppermute | solution.py:320
  246.7 11.2 %collective-permute-done.7.refs_2_ = f32[512,256]{1,0:T(8,128)S(1)} collective-permute-done((f32[512,256]{1,0:T(8,128)S(1)}, f32[512,256]{1,0:T(8,128)S(1)}, u32[]{:S(2)}, u32[]{:S(2)}) %collective-permute-start.7) | collective-permute-done | bytes 524320 | tf_op jit(solution)/shard_map/ppermute | solution.py:320
  259.6 5.6 %stack_for_holders.2 = f32[8,512,256]{2,1,0:T(8,128)} custom-call(s32[2]{0:T(128)} %pad_add_fusion.ids_ref, s32[32]{0:T(128)} %table_ref.15, f32[512,256]{1,0:T(8,128)} %convolution_select_fusion.3.refs_0_, f32[512,256]{1,0:T(8,128)} %copy-done.10, f32[512,256]{1,0:T(8,128)} %copy-done.11, f32[512,256]{1,0:T(8,128)} %copy-done.12), custom_call_target="tpu_custom_call" | custom-call | tf_op jit(solution)/shard_map/stack_for_holders/pallas_call | solution.py:241
  266.3 4.9 %all-to-all-start.1 = ((f32[8,512,256]{2,1,0:T(8,128)}), f32[8,512,256]{2,1,0:T(8,128)}, u32[]{:S(2)}, u32[]{:S(2)}) async-start(f32[8,512,256]{2,1,0:T(8,128)} %stack_for_holders.2), calls=%async_computation.1 | async-start | bytes 8388608 | tf_op jit(solution)/shard_map/all_to_all | solution.py:324
  271.2 4.7 %adam.1 = (f32[4,64,768]{2,1,0:T(8,128)}, f32[4,64,768]{2,1,0:T(8,128)}, f32[4,64,768]{2,1,0:T(8,128)}) custom-call(s32[2]{0:T(128)} %pad_add_fusion.ids_ref, s32[32]{0:T(128)} %table_ref.15, f32[8,64,768]{2,1,0:T(8,128)} %all-to-all-done.2.proj_ref, f32[4,64,768]{2,1,0:T(8,128)} %one_ref.1, f32[4,64,768]{2,1,0:T(8,128)} %two_ref.1), custom_call_target="tpu_custom_call" | custom-call | tf_op jit(solution)/shard_map/adam/pallas_call | solution.py:267
  275.9 31.0 %all-gather.2.cloned.1.call-done.normed_ref = f32[4,256,768]{2,1,0:T(8,128)} async-done(((f32[4,64,768]{2,1,0:T(8,128)}), f32[4,256,768]{2,1,0:T(8,128)}) %all-gather.2.cloned.1.call-update) | async-done | bytes 3145744 | tf_op jit(solution)/shard_map/all_gather | solution.py:374
  306.9 57.8 %all-to-all-done.1.basis_ref = f32[8,512,256]{2,1,0:T(8,128)} async-done(((f32[8,512,256]{2,1,0:T(8,128)}), f32[8,512,256]{2,1,0:T(8,128)}, u32[]{:S(2)}, u32[]{:S(2)}) %all-to-all-start.1) | async-done | bytes 4194336 | tf_op jit(solution)/shard_map/all_to_all | solution.py:324
  364.7 7.2 %updates.1 = (f32[4,512,256]{2,1,0:T(8,128)}, bf16[4,512,768]{2,1,0:T(8,128)(2,1)}) custom-call(s32[2]{0:T(128)} %pad_add_fusion.ids_ref, s32[32]{0:T(128)} %table_ref.15, f32[8,512,256]{2,1,0:T(8,128)} %all-to-all-done.1.basis_ref, f32[4,256,768]{2,1,0:T(8,128)} %all-gather.2.cloned.1.call-done.normed_ref), custom_call_target="tpu_custom_call" | custom-call | tf_op jit(solution)/shard_map/updates/pallas_call | solution.py:294
  (60 shorter events, 15.3 us)
Async XLA Ops:
  15.1 100.8 %all-to-all-start = ((f32[8,512,256]{2,1,0:T(8,128)}), f32[8,512,256]{2,1,0:T(8,128)}, u32[]{:S(2)}, u32[]{:S(2)}) async-start(f32[8,512,256]{2,1,0:T(8,128)} %pick_stack.1), calls=%async_computation | async-start | bytes 8388608 | tf_op jit(solution)/shard_map/all_to_all | solution.py:324
  22.6 8.7 %copy-start.17 = (s32[32]{0:T(128)S(1)}, s32[32]{0:T(128)}, u32[]{:S(2)}) copy-start(s32[32]{0:T(128)} %param.11) | copy-start | bytes 388
  28.1 37.5 %collective-permute-start.1 = (f32[512,768]{1,0:T(8,128)}, f32[512,768]{1,0:T(8,128)S(1)}, u32[]{:S(2)}, u32[]{:S(2)}) collective-permute-start(f32[512,768]{1,0:T(8,128)} %get-tuple-element.25), channel_id=1, source_target_pairs={{0,16},{8,24},{16,0},{24,8},{1,17},{9,25},{17,1},{25,9},{2,18},{10... | collective-permute-start | bytes 4718600 | tf_op jit(solution)/shard_map/ppermute | solution.py:320
  29.6 66.9 %collective-permute-start = (f32[512,768]{1,0:T(8,128)}, f32[512,768]{1,0:T(8,128)S(1)}, u32[]{:S(2)}, u32[]{:S(2)}) collective-permute-start(f32[512,768]{1,0:T(8,128)} %get-tuple-element.24), channel_id=1, source_target_pairs={{0,8},{8,16},{16,24},{24,0},{1,9},{9,17},{17,25},{25,1},{2,10},{10... | collective-permute-start | bytes 4718600 | tf_op jit(solution)/shard_map/ppermute | solution.py:320
  29.6 89.8 %collective-permute-start.2 = (f32[512,768]{1,0:T(8,128)}, f32[512,768]{1,0:T(8,128)}, u32[]{:S(2)}, u32[]{:S(2)}) collective-permute-start(f32[512,768]{1,0:T(8,128)} %get-tuple-element.26), channel_id=1, source_target_pairs={{0,24},{8,0},{16,8},{24,16},{1,25},{9,1},{17,9},{25,17},{2,26},{10... | collective-permute-start | bytes 4718600 | tf_op jit(solution)/shard_map/ppermute | solution.py:320
  119.2 8.1 %copy-start.16 = (f32[512,256]{1,0:T(8,128)S(1)}, f32[512,256]{1,0:T(8,128)}, u32[]{:S(2)}) copy-start(f32[512,256]{1,0:T(8,128)} %get-tuple-element.28) | copy-start | bytes 1572868
  119.2 8.4 %copy-start.15 = (f32[512,256]{1,0:T(8,128)S(1)}, f32[512,256]{1,0:T(8,128)}, u32[]{:S(2)}) copy-start(f32[512,256]{1,0:T(8,128)} %get-tuple-element.29) | copy-start | bytes 1572868
  119.3 9.9 %copy-start = (f32[512,768]{1,0:T(8,128)S(1)}, f32[512,768]{1,0:T(8,128)}, u32[]{:S(2)}) copy-start(f32[512,768]{1,0:T(8,128)} %get-tuple-element.23) | copy-start | bytes 4718596
  119.3 9.9 %copy-start.6 = (f32[512,256]{1,0:T(8,128)S(1)}, f32[512,256]{1,0:T(8,128)}, u32[]{:S(2)}) copy-start(f32[512,256]{1,0:T(8,128)} %get-tuple-element.27) | copy-start | bytes 1572868
  119.3 10.9 %collective-permute-start.5 = (f32[512,256]{1,0:T(8,128)}, f32[512,256]{1,0:T(8,128)S(1)}, u32[]{:S(2)}, u32[]{:S(2)}) collective-permute-start(f32[512,256]{1,0:T(8,128)} %get-tuple-element.30), channel_id=1, source_target_pairs={{0,24},{8,0},{16,8},{24,16},{1,25},{9,1},{17,9},{25,17},{2,26},{10... | collective-permute-start | bytes 1572872 | tf_op jit(solution)/shard_map/ppermute | solution.py:320
  127.3 13.3 %collective-permute-start.3 = (f32[512,256]{1,0:T(8,128)S(1)}, f32[512,256]{1,0:T(8,128)S(1)}, u32[]{:S(2)}, u32[]{:S(2)}) collective-permute-start(f32[512,256]{1,0:T(8,128)S(1)} %copy-done.16), channel_id=1, source_target_pairs={{0,8},{8,16},{16,24},{24,0},{1,9},{9,17},{17,25},{25,1},{2,10},{10... | collective-permute-start | bytes 1572872 | tf_op jit(solution)/shard_map/ppermute | solution.py:320
  127.7 14.8 %collective-permute-start.4 = (f32[512,256]{1,0:T(8,128)S(1)}, f32[512,256]{1,0:T(8,128)S(1)}, u32[]{:S(2)}, u32[]{:S(2)}) collective-permute-start(f32[512,256]{1,0:T(8,128)S(1)} %copy-done.15), channel_id=1, source_target_pairs={{0,16},{8,24},{16,0},{24,8},{1,17},{9,25},{17,1},{25,9},{2,18},{10... | collective-permute-start | bytes 1572872 | tf_op jit(solution)/shard_map/ppermute | solution.py:320
  130.1 11.4 %copy-start.8 = (f32[512,256]{1,0:T(8,128)}, f32[512,256]{1,0:T(8,128)S(1)}, u32[]{:S(2)}) copy-start(f32[512,256]{1,0:T(8,128)S(1)} %collective-permute-done.5) | copy-start | bytes 1572868
  140.7 0.9 copy-start.5
  164.1 11.2 %collective-permute-start.9 = (f32[64,768]{1,0:T(8,128)}, f32[64,768]{1,0:T(8,128)S(1)}, u32[]{:S(2)}, u32[]{:S(2)}) collective-permute-start(f32[64,768]{1,0:T(8,128)} %get-tuple-element.34), channel_id=1, source_target_pairs={{0,24},{8,0},{16,8},{24,16},{1,25},{9,1},{17,9},{25,17},{2,26},{10... | collective-permute-start | bytes 589832 | tf_op jit(solution)/shard_map/ppermute | solution.py:320
  169.8 10.1 %collective-permute-start.10 = (f32[64,768]{1,0:T(8,128)}, f32[64,768]{1,0:T(8,128)S(1)}, u32[]{:S(2)}, u32[]{:S(2)}) collective-permute-start(f32[64,768]{1,0:T(8,128)} %get-tuple-element.35), channel_id=1, source_target_pairs={{0,16},{8,24},{16,0},{24,8},{1,17},{9,25},{17,1},{25,9},{2,18},{10... | collective-permute-start | bytes 589832 | tf_op jit(solution)/shard_map/ppermute | solution.py:320
  170.3 9.6 %collective-permute-start.11 = (f32[64,768]{1,0:T(8,128)}, f32[64,768]{1,0:T(8,128)}, u32[]{:S(2)}, u32[]{:S(2)}) collective-permute-start(f32[64,768]{1,0:T(8,128)} %get-tuple-element.36), channel_id=1, source_target_pairs={{0,8},{8,16},{16,24},{24,0},{1,9},{9,17},{17,25},{25,1},{2,10},{10... | collective-permute-start | bytes 589832 | tf_op jit(solution)/shard_map/ppermute | solution.py:320
  175.4 4.5 %copy-start.13 = (f32[64,768]{1,0:T(8,128)}, f32[64,768]{1,0:T(8,128)S(1)}, u32[]{:S(2)}) copy-start(f32[64,768]{1,0:T(8,128)S(1)} %collective-permute-done.9.refs_1_) | copy-start | bytes 589828
  184.2 82.1 %all-to-all-start.2 = ((f32[8,64,768]{2,1,0:T(8,128)}), f32[8,64,768]{2,1,0:T(8,128)}, u32[]{:S(2)}, u32[]{:S(2)}) async-start(f32[8,64,768]{2,1,0:T(8,128)} %stack_for_holders.3), calls=%async_computation.2 | async-start | bytes 3145728 | tf_op jit(solution)/shard_map/all_to_all | solution.py:324
  233.0 2.2 copy-start.2
  233.0 2.2 copy-start.4
  235.1 1.0 copy-start.9
  235.1 11.6 %collective-permute-start.6 = (f32[512,256]{1,0:T(8,128)S(1)}, f32[512,256]{1,0:T(8,128)S(1)}, u32[]{:S(2)}, u32[]{:S(2)}) collective-permute-start(f32[512,256]{1,0:T(8,128)S(1)} %convolution_select_fusion.2), channel_id=1, source_target_pairs={{0,24},{8,0},{16,8},{24,16},{1,25},{9,1},{17,9},{25,17},{2,26},{10... | collective-permute-start | bytes 1572872 | tf_op jit(solution)/shard_map/ppermute | solution.py:320
  236.0 3.0 copy-start.1
  236.0 3.0 copy-start.7
  236.0 21.9 %collective-permute-start.7 = (f32[512,256]{1,0:T(8,128)S(1)}, f32[512,256]{1,0:T(8,128)S(1)}, u32[]{:S(2)}, u32[]{:S(2)}) collective-permute-start(f32[512,256]{1,0:T(8,128)S(1)} %convolution_select_fusion.1), channel_id=1, source_target_pairs={{0,16},{8,24},{16,0},{24,8},{1,17},{9,25},{17,1},{25,9},{2,18},{10... | collective-permute-start | bytes 1572872 | tf_op jit(solution)/shard_map/ppermute | solution.py:320
  238.5 20.3 %collective-permute-start.8 = (f32[512,256]{1,0:T(8,128)S(1)}, f32[512,256]{1,0:T(8,128)S(1)}, u32[]{:S(2)}, u32[]{:S(2)}) collective-permute-start(f32[512,256]{1,0:T(8,128)S(1)} %convolution_select_fusion), channel_id=1, source_target_pairs={{0,8},{8,16},{16,24},{24,0},{1,9},{9,17},{17,25},{25,1},{2,10},{10... | collective-permute-start | bytes 1572872 | tf_op jit(solution)/shard_map/ppermute | solution.py:320
  246.7 11.2 %copy-start.10 = (f32[512,256]{1,0:T(8,128)}, f32[512,256]{1,0:T(8,128)S(1)}, u32[]{:S(2)}) copy-start(f32[512,256]{1,0:T(8,128)S(1)} %collective-permute-done.6.refs_1_) | copy-start | bytes 1572868
  258.0 0.8 copy-start.11
  258.8 0.8 copy-start.12
  266.3 98.4 %all-to-all-start.1 = ((f32[8,512,256]{2,1,0:T(8,128)}), f32[8,512,256]{2,1,0:T(8,128)}, u32[]{:S(2)}, u32[]{:S(2)}) async-start(f32[8,512,256]{2,1,0:T(8,128)} %stack_for_holders.2), calls=%async_computation.1 | async-start | bytes 8388608 | tf_op jit(solution)/shard_map/all_to_all | solution.py:324
  271.2 35.7 %all-gather.2.cloned.1.call-start = ((), (), s32[]{:S(2)}) async-start(), calls=%async_computation.3 | async-start | bytes 3932160 | tf_op jit(solution)/shard_map/all_gather | solution.py:374
  (2 other events, 1.5 us)
Sparse Core Ops, SparseCore 0:
  276.0 30.8 all-gather.1
